TPU v7x, 32 devices: a whole 2x2x4 slice. The times are simulated.
32 devices in a mesh: pp: 4 (over x, core), tp: 2 (over y), dp: 4 (over z).
Axes of the slice: x: 2, y: 2, z: 4, core: 2. Of those that a mesh axis runs over, the one named last changes fastest.
Arguments:
- layer_input: bfloat16 [4, 4, 16, 4096], P('pp', 'dp', 'tp'), may hold values from -4 to 4
- gate_pre: bfloat16 [4, 4, 16, 14784], P('pp', 'dp', None, 'tp'), may hold values from -8 to 8
- up_pre: bfloat16 [4, 4, 16, 14784], P('pp', 'dp', None, 'tp'), may hold values from -6 to 6
- hidden_grad: bfloat16 [4, 4, 16, 14784], P('pp', 'dp', None, 'tp'), may hold values from -0.59765625 to 0.59765625
- gate_weight: bfloat16 [4, 4096, 14784], P('pp', 'dp', 'tp'), may hold values from -0.09375 to 0.09375
Outputs:
- passed_grad: bfloat16 [4, 4, 16, 4096], P('pp', 'dp', 'tp')
- gate_weight_grad: bfloat16 [4, 4096, 14784], P('pp', 'dp', 'tp')
All inputs are finite; a program needn't handle non-finite values.
Results may differ from a plain program's by a relative error of at most 0.018.
Values may be sent and summed in bfloat16 or wider, within the bound.
No kernel may reach another device: no remote copies, remote signals or barrier semaphores. Data moves between devices by JAX's collectives and lax.ppermute only.
A program may use at most 128 MiB of HBM per device.

v0:
```python
import jax
import jax.numpy as jnp
from jax import lax
from jax.sharding import PartitionSpec as P


def from_behind(block, axis, distance):
    devices = range(lax.axis_size(axis))
    route = [(i - distance, i) for i in devices if i - distance in devices]
    return lax.ppermute(block, axis, route)


def finish(partial_value):
    return lax.psum_scatter(
        partial_value.astype(jnp.bfloat16), "tp", scatter_dimension=0, tiled=True
    )


def on_device(layer_input, gate_pre, up_pre, hidden_grad, gate_weight):
    tokens_in = layer_input[0, 0]
    gate_val = gate_pre[0, 0].astype(jnp.float32)
    up_val = up_pre[0, 0].astype(jnp.float32)
    hidden_val = hidden_grad[0, 0].astype(jnp.float32)
    gate_local = gate_weight[0]
    rows_total = gate_val.shape[0]
    groups = lax.axis_size("dp")
    logistic = jax.nn.sigmoid(gate_val)
    gate_grad = (hidden_val * up_val * logistic * (1.0 + gate_val * (1.0 - logistic))).astype(
        jnp.bfloat16
    )
    gathered_in = lax.all_gather(tokens_in, "tp", axis=0, tiled=True)
    contract_cols = (((1,), (1,)), ((), ()))
    all_grads = lax.all_gather(gate_grad, "dp", axis=0, tiled=True)
    partial_value = lax.dot_general(
        all_grads, gate_local, contract_cols, preferred_element_type=jnp.float32
    )
    returned = lax.all_to_all(
        partial_value.astype(jnp.bfloat16), "dp", split_axis=0, concat_axis=1, tiled=True
    ).astype(partial_value.dtype)
    input_grad = finish(returned)
    in_columns = lax.all_to_all(gathered_in, "dp", split_axis=1, concat_axis=0, tiled=True)
    products = lax.dot_general(
        in_columns.reshape(groups, rows_total, in_columns.shape[1]),
        all_grads.reshape(groups, rows_total, all_grads.shape[1]),
        (((1,), (1,)), ((0,), (0,))),
        preferred_element_type=jnp.float32,
    )
    rounded = lax.optimization_barrier(products.astype(jnp.bfloat16))
    grads_total = jnp.sum(rounded.astype(jnp.float32), axis=0)
    passed = from_behind(input_grad, "pp", -1)
    gate_out = grads_total.astype(jnp.bfloat16)
    return (passed[None, None], gate_out[None])


def solution(mesh):
    return jax.shard_map(
        on_device,
        mesh=mesh,
        in_specs=(
            P("pp", "dp", "tp", None),
            P("pp", "dp", None, "tp"),
            P("pp", "dp", None, "tp"),
            P("pp", "dp", None, "tp"),
            P("pp", "dp", "tp"),
        ),
        out_specs=(P("pp", "dp", "tp", None), P("pp", "dp", "tp")),
        check_vma=False,
    )
```

profile of v0, /device:TPU:0, one launch (start us, length us, event | category | flops | bytes accessed | tf_op | source)
XLA Modules:
  0.0 123.4 jit_solution(5903681675003052307)
XLA Ops:
  7.2 0.0 copy-start
  7.2 0.0 reduce-scatter.2.cloned.1.call-start
  7.2 1.4 %fusion.10 = bf16[16,7392]{1,0:T(8,128)(2,1)S(1)} fusion(bf16[1,1,16,7392]{3,2,1,0:T(8,128)(2,1)} %param.7, bf16[1,1,16,7392]{3,2,1,0:T(8,128)(2,1)} %param.8, bf16[1,1,16,7392]{3,2,1,0:T(8,128)(2,1)} %param.6), kind=kLoop, calls=%fused_computation.11 | loop fusion | flops 1537536 | bytes 946176 | tf_op jit(solution)/shard_map/convert_element_type | solution.py:28
  8.6 23.1 %all_gather.6 = bf16[64,7392]{1,0:T(8,128)(2,1)S(1)} all-gather(bf16[16,7392]{1,0:T(8,128)(2,1)S(1)} %fusion.10), channel_id=1, replica_groups=mesh['pp'=4,'tp'=2,'dp'=4] {'dp'}, dimensions={0}, use_global_device_ids=true | all-gather | bytes 1182720 | tf_op jit(solution)/shard_map/all_gather | solution.py:33
  31.7 8.0 %fusion.2 = bf16[64,1024]{1,0:T(8,128)(2,1)S(1)} fusion(bf16[64,7392]{1,0:T(8,128)(2,1)S(1)} %all_gather.6, bf16[1,1024,7392]{1,2,0:T(8,128)(2,1)} %param.9), kind=kOutput, calls=%fused_computation.3 | convolution fusion | flops 968949760 | bytes 16216064 | tf_op jit(solution)/shard_map/dot_general | solution.py:34
  39.8 9.1 %all_to_all.35 = bf16[4,16,1024]{2,1,0:T(8,128)(2,1)S(1)} all-to-all(bf16[4,16,1024]{2,1,0:T(8,128)(2,1)S(1)} %bitcast.30), channel_id=1, replica_groups=mesh['pp'=4,'tp'=2,'dp'=4] {'dp'}, dimensions={0} | all-to-all | bytes 262144 | tf_op jit(solution)/shard_map/all_to_all | solution.py:37
  48.9 0.7 copy.10
  49.5 0.0 reduce-scatter.2.cloned.1.call-update
  49.6 0.0 copy-done
  49.6 4.9 %all-gather = bf16[1,1,16,4096]{3,2,1,0:T(8,128)(2,1)S(1)} all-gather(bf16[1,1,8,4096]{3,2,1,0:T(8,128)(2,1)S(1)} %copy-done), channel_id=2, replica_groups=mesh['pp'=4,'tp'=2,'dp'=4] {'tp'}, dimensions={2}, use_global_device_ids=true | all-gather | bytes 196608 | tf_op jit(solution)/shard_map/all_gather | solution.py:31
  54.5 0.1 all_to_all.30
  54.6 0.7 copy.9
  55.3 3.3 %all-to-all-start.1 = ((bf16[16,4,1024]{2,0,1:T(8,128)(2,1)}), bf16[16,4,1024]{2,0,1:T(8,128)(2,1)S(1)}, u32[]{:S(2)}, u32[]{:S(2)}) async-start(bf16[16,4,1024]{2,0,1:T(8,128)(2,1)} %copy.9), calls=%async_computation.2 | async-start | bytes 262144 | tf_op jit(solution)/shard_map/all_to_all | solution.py:41
  58.6 0.5 reduce-scatter.2.cloned.1.call-done
  59.1 1.3 %collective-permute-start = (bf16[8,4096]{1,0:T(8,128)(2,1)}, bf16[8,4096]{1,0:T(8,128)(2,1)S(1)}, u32[]{:S(2)}, u32[]{:S(2)}) collective-permute-start(bf16[8,4096]{1,0:T(8,128)(2,1)} %reduce-scatter.2.cloned.1.call-done), channel_id=1, source_target_pairs={{8,0},{16,8},{24,16},{9,1},{17,9},{25,17},{10,2},{18,10},{26,18},{... | collective-permute-start | bytes 196616 | tf_op jit(solution)/shard_map/ppermute | solution.py:10
  60.4 4.1 %all-to-all-done.1 = bf16[16,4,1024]{2,0,1:T(8,128)(2,1)S(1)} async-done(((bf16[16,4,1024]{2,0,1:T(8,128)(2,1)}), bf16[16,4,1024]{2,0,1:T(8,128)(2,1)S(1)}, u32[]{:S(2)}, u32[]{:S(2)}) %all-to-all-start.1) | async-done | bytes 131104 | tf_op jit(solution)/shard_map/all_to_all | solution.py:41
  64.5 23.4 %convert_bitcast_fusion = bf16[4,1024,7392]{1,2,0:T(8,128)(2,1)} fusion(bf16[4,16,7392]{2,1,0:T(8,128)(2,1)S(1)} %bitcast.28, bf16[16,4,1024]{2,0,1:T(8,128)(2,1)S(1)} %all-to-all-done.1), kind=kOutput, calls=%fused_computation | convolution fusion | flops 999161856 | bytes 61632512 | tf_op jit(solution)/shard_map/dot_general | solution.py:42
  87.9 28.0 %reduce_sum.12 = bf16[1024,7392]{0,1:T(8,128)(2,1)} reduce(bf16[4,1024,7392]{1,2,0:T(8,128)(2,1)} %convert_bitcast_fusion, bf16[]{:T(256)} %constant.4.clone.1), dimensions={0}, to_apply=%region_1.0 | reduce | flops 22708224 | bytes 75694080 | tf_op jit(solution)/shard_map/reduce_sum | solution.py:49
  115.9 0.0 collective-permute-done
  115.9 0.6 copy.12
Async XLA Ops:
  7.2 42.4 %copy-start = (bf16[1,1,8,4096]{3,2,1,0:T(8,128)(2,1)S(1)}, bf16[1,1,8,4096]{3,2,1,0:T(8,128)(2,1)}, u32[]{:S(2)}) copy-start(bf16[1,1,8,4096]{3,2,1,0:T(8,128)(2,1)} %param.5) | copy-start | bytes 196612
  7.2 51.9 %reduce-scatter.2.cloned.1.call-start = ((), (), s32[]{:S(2)}) async-start(), calls=%async_computation.3 | async-start | bytes 196608 | tf_op jit(solution)/shard_map/reduce_scatter | solution.py:14
  55.3 9.2 %all-to-all-start.1 = ((bf16[16,4,1024]{2,0,1:T(8,128)(2,1)}), bf16[16,4,1024]{2,0,1:T(8,128)(2,1)S(1)}, u32[]{:S(2)}, u32[]{:S(2)}) async-start(bf16[16,4,1024]{2,0,1:T(8,128)(2,1)} %copy.9), calls=%async_computation.2 | async-start | bytes 262144 | tf_op jit(solution)/shard_map/all_to_all | solution.py:41
  59.1 56.8 %collective-permute-start = (bf16[8,4096]{1,0:T(8,128)(2,1)}, bf16[8,4096]{1,0:T(8,128)(2,1)S(1)}, u32[]{:S(2)}, u32[]{:S(2)}) collective-permute-start(bf16[8,4096]{1,0:T(8,128)(2,1)} %reduce-scatter.2.cloned.1.call-done), channel_id=1, source_target_pairs={{8,0},{16,8},{24,16},{9,1},{17,9},{25,17},{10,2},{18,10},{26,18},{... | collective-permute-start | bytes 196616 | tf_op jit(solution)/shard_map/ppermute | solution.py:10
Sparse Core Ops, SparseCore 0:
  49.7 9.3 reduce-scatter.1
where the time goes:
time: 124 us; the launch traced here: 123 us
  blocking collectives  37.1 us (30%)
  matrix products  31.5 us (25%)
  other arithmetic  29.4 us (24%)
  between operations  14.1 us (11%)
  starting transfers between devices  4.64 us (4%)
  waiting for transfers between devices  4.62 us (4%)
  local copies, waits for them, and re-layouts  2.05 us (2%)
    reduce_sum x1, other arithmetic, on_device(): grads_total = jnp.sum(rounded.astype(jnp.float32), axis=0)  28 us
    dot_general x1, matrix products, on_device(): lax.dot_general(in_columns.reshape(groups, rows_total, in_columns.shape[1...  23.4 us
    all_gather x1, blocking collectives, on_device(): all_grads = lax.all_gather(gate_grad, 'dp', axis=0, tiled=True)  23.1 us
    all_to_all x1, blocking collectives, on_device(): lax.all_to_all(partial_value.astype(jnp.bfloat16), 'dp', split_axis=0, co...  9.09 us
    dot_general x1, matrix products, on_device(): lax.dot_general(all_grads, gate_local, contract_cols, preferred_element_t...  8.04 us
    all_gather x1, blocking collectives, on_device(): gathered_in = lax.all_gather(tokens_in, 'tp', axis=0, tiled=True)  4.93 us
    all_to_all x1, waiting for transfers between devices, on_device(): lax.all_to_all(gathered_in, 'dp', split_axis=1, concat_axis=0, tiled=True)  4.06 us
    all_to_all x1, starting transfers between devices, on_device(): lax.all_to_all(gathered_in, 'dp', split_axis=1, concat_axis=0, tiled=True)  3.32 us
  transfers between devices with their start and end apart: 3, of which 2 were waited for; matrix products, arithmetic and copies ran while one was open for 42% of the time, Pallas kernels for 0%

commit v1 on v0

--- a/solution.py
+++ b/solution.py
@@ -30,7 +30,21 @@
     )
     gathered_in = lax.all_gather(tokens_in, "tp", axis=0, tiled=True)
     contract_cols = (((1,), (1,)), ((), ()))
-    all_grads = lax.all_gather(gate_grad, "dp", axis=0, tiled=True)
+
+    def take_joints(m, peer_axis="dp"):
+        chips = lax.axis_size(peer_axis)
+        u_next = sorted(((dev_i, (dev_i + 1) % chips) for dev_i in range(chips)))
+        later = m
+        row_list = [later]
+        for hop_no in range(1, chips):
+            later = lax.ppermute(later, peer_axis, u_next)
+            row_list.insert(0, later)
+        parts_out = jnp.concatenate(row_list, 0)
+        block_out = lax.axis_index(peer_axis)
+        far_arr = block_out + 1
+        return jnp.roll(parts_out, far_arr * m.shape[0], 0)
+
+    all_grads = take_joints(gate_grad)
     partial_value = lax.dot_general(
         all_grads, gate_local, contract_cols, preferred_element_type=jnp.float32
     )

time: 124 us -> 128 us (1.032)
  waiting for transfers between devices: 4.62 us -> 29.1 us
  blocking collectives: 37.1 us -> 13.2 us
  starting transfers between devices: 4.64 us -> 7.75 us
    ppermute x0 -> x3, waiting for transfers between devices: none -> 24.4 us  [take_joints(): later = lax.ppermute(later, peer_axis, u_next)]
    all_gather x1 -> x0, blocking collectives: 23.1 us -> none  [on_device(): all_grads = lax.all_gather(gate_grad, 'dp', axis=0, tiled=True)]
    ppermute x0 -> x3, starting transfers between devices: none -> 3.11 us  [take_joints(): later = lax.ppermute(later, peer_axis, u_next)]
  transfers between devices with their start and end apart: 3 -> 6, of which waited for: 2 -> 5; matrix products, arithmetic and copies ran while one was open for 42% -> 41% of each run, Pallas kernels for 0% -> 0%
where the time goes in v1:
time: 128 us; the launch traced here: 127 us
  matrix products  31.5 us (25%)
  other arithmetic  29.4 us (23%)
  waiting for transfers between devices  29.1 us (23%)
  between operations  14.1 us (11%)
  blocking collectives  13.2 us (10%)
  starting transfers between devices  7.75 us (6%)
  local copies, waits for them, and re-layouts  2.28 us (2%)
    reduce_sum x1, other arithmetic, on_device(): grads_total = jnp.sum(rounded.astype(jnp.float32), axis=0)  28 us
    ppermute x3, waiting for transfers between devices, take_joints(): later = lax.ppermute(later, peer_axis, u_next)  24.4 us
    dot_general x1, matrix products, on_device(): lax.dot_general(in_columns.reshape(groups, rows_total, in_columns.shape[1...  23.4 us
    all_to_all x1, blocking collectives, on_device(): lax.all_to_all(partial_value.astype(jnp.bfloat16), 'dp', split_axis=0, co...  8.31 us
    dot_general x1, matrix products, on_device(): lax.dot_general(all_grads, gate_local, contract_cols, preferred_element_t...  8.08 us
    all_gather x1, blocking collectives, on_device(): gathered_in = lax.all_gather(tokens_in, 'tp', axis=0, tiled=True)  4.93 us
    all_to_all x1, waiting for transfers between devices, on_device(): lax.all_to_all(gathered_in, 'dp', split_axis=1, concat_axis=0, tiled=True)  4.28 us
    all_to_all x1, starting transfers between devices, on_device(): lax.all_to_all(gathered_in, 'dp', split_axis=1, concat_axis=0, tiled=True)  3.32 us
  transfers between devices with their start and end apart: 6, of which 5 were waited for; matrix products, arithmetic and copies ran while one was open for 41% of the time, Pallas kernels for 0%

profile of v1, /device:TPU:0, one launch (start us, length us, event | category | flops | bytes accessed | tf_op | source)
XLA Modules:
  0.0 127.4 jit_solution(12091201179701221902)
XLA Ops:
  7.2 0.0 reduce-scatter.2.cloned.1.call-start
  7.2 1.4 %fusion.10 = bf16[16,7392]{1,0:T(8,128)(2,1)S(1)} fusion(bf16[1,1,16,7392]{3,2,1,0:T(8,128)(2,1)} %param.7, bf16[1,1,16,7392]{3,2,1,0:T(8,128)(2,1)} %param.8, bf16[1,1,16,7392]{3,2,1,0:T(8,128)(2,1)} %param.6), kind=kLoop, calls=%fused_computation.11 | loop fusion | flops 1537536 | bytes 946176 | tf_op jit(solution)/shard_map/convert_element_type | solution.py:28
  8.6 3.1 %collective-permute-start = (bf16[16,7392]{1,0:T(8,128)(2,1)S(1)}, bf16[16,7392]{1,0:T(8,128)(2,1)S(1)}, u32[]{:S(2)}, u32[]{:S(2)}) collective-permute-start(bf16[16,7392]{1,0:T(8,128)(2,1)S(1)} %fusion.10), channel_id=1, source_target_pairs={{0,1},{1,2},{2,3},{3,0},{4,5},{5,6},{6,7},{7,4},{8,9},{9,10},{10,1... | collective-permute-start | bytes 709640 | tf_op jit(solution)/shard_map/ppermute | solution.py:40
  11.7 7.8 %collective-permute-done = bf16[16,7392]{1,0:T(8,128)(2,1)S(1)} collective-permute-done((bf16[16,7392]{1,0:T(8,128)(2,1)S(1)}, bf16[16,7392]{1,0:T(8,128)(2,1)S(1)}, u32[]{:S(2)}, u32[]{:S(2)}) %collective-permute-start) | collective-permute-done | bytes 236576 | tf_op jit(solution)/shard_map/ppermute | solution.py:40
  19.5 0.0 collective-permute-start.1
  19.5 8.7 %collective-permute-done.1 = bf16[16,7392]{1,0:T(8,128)(2,1)S(1)} collective-permute-done((bf16[16,7392]{1,0:T(8,128)(2,1)S(1)}, bf16[16,7392]{1,0:T(8,128)(2,1)S(1)}, u32[]{:S(2)}, u32[]{:S(2)}) %collective-permute-start.1) | collective-permute-done | bytes 236576 | tf_op jit(solution)/shard_map/ppermute | solution.py:40
  28.3 0.0 collective-permute-start.2
  28.3 7.9 %collective-permute-done.2 = bf16[16,7392]{1,0:T(8,128)(2,1)S(1)} collective-permute-done((bf16[16,7392]{1,0:T(8,128)(2,1)S(1)}, bf16[16,7392]{1,0:T(8,128)(2,1)S(1)}, u32[]{:S(2)}, u32[]{:S(2)}) %collective-permute-start.2) | collective-permute-done | bytes 236576 | tf_op jit(solution)/shard_map/ppermute | solution.py:40
  36.4 0.1 constant_dynamic-slice_fusion
  36.4 0.0 copy-start
  36.5 8.1 %fusion.2 = bf16[64,1024]{1,0:T(8,128)(2,1)S(1)} fusion(bf16[64,7392]{1,0:T(8,128)(2,1)S(1)} %constant_dynamic-slice_fusion, bf16[1,1024,7392]{1,2,0:T(8,128)(2,1)} %param.9), kind=kOutput, calls=%fused_computation.3 | convolution fusion | flops 968949760 | bytes 16216064 | tf_op jit(solution)/shard_map/dot_general | solution.py:48
  44.5 8.3 %all_to_all.35 = bf16[4,16,1024]{2,1,0:T(8,128)(2,1)S(1)} all-to-all(bf16[4,16,1024]{2,1,0:T(8,128)(2,1)S(1)} %bitcast.30), channel_id=1, replica_groups=mesh['pp'=4,'tp'=2,'dp'=4] {'dp'}, dimensions={0} | all-to-all | bytes 262144 | tf_op jit(solution)/shard_map/all_to_all | solution.py:51
  52.8 0.7 copy.10
  53.5 0.0 reduce-scatter.2.cloned.1.call-update
  53.5 0.0 copy-done
  53.5 4.9 %all-gather = bf16[1,1,16,4096]{3,2,1,0:T(8,128)(2,1)S(1)} all-gather(bf16[1,1,8,4096]{3,2,1,0:T(8,128)(2,1)S(1)} %copy-done), channel_id=2, replica_groups=mesh['pp'=4,'tp'=2,'dp'=4] {'tp'}, dimensions={2}, use_global_device_ids=true | all-gather | bytes 196608 | tf_op jit(solution)/shard_map/all_gather | solution.py:31
  58.5 0.1 all_to_all.30
  58.6 0.7 copy.9
  59.2 3.3 %all-to-all-start.1 = ((bf16[16,4,1024]{2,0,1:T(8,128)(2,1)}), bf16[16,4,1024]{2,0,1:T(8,128)(2,1)S(1)}, u32[]{:S(2)}, u32[]{:S(2)}) async-start(bf16[16,4,1024]{2,0,1:T(8,128)(2,1)} %copy.9), calls=%async_computation.2 | async-start | bytes 262144 | tf_op jit(solution)/shard_map/all_to_all | solution.py:55
  62.6 0.3 reduce-scatter.2.cloned.1.call-done
  62.9 1.3 %collective-permute-start.3 = (bf16[8,4096]{1,0:T(8,128)(2,1)}, bf16[8,4096]{1,0:T(8,128)(2,1)S(1)}, u32[]{:S(2)}, u32[]{:S(2)}) collective-permute-start(bf16[8,4096]{1,0:T(8,128)(2,1)} %reduce-scatter.2.cloned.1.call-done), channel_id=1, source_target_pairs={{8,0},{16,8},{24,16},{9,1},{17,9},{25,17},{10,2},{18,10},{26,18},{... | collective-permute-start | bytes 196616 | tf_op jit(solution)/shard_map/ppermute | solution.py:10
  64.2 4.3 %all-to-all-done.1 = bf16[16,4,1024]{2,0,1:T(8,128)(2,1)S(1)} async-done(((bf16[16,4,1024]{2,0,1:T(8,128)(2,1)}), bf16[16,4,1024]{2,0,1:T(8,128)(2,1)S(1)}, u32[]{:S(2)}, u32[]{:S(2)}) %all-to-all-start.1) | async-done | bytes 131104 | tf_op jit(solution)/shard_map/all_to_all | solution.py:55
  68.5 23.4 %convert_bitcast_fusion = bf16[4,1024,7392]{1,2,0:T(8,128)(2,1)} fusion(bf16[4,16,7392]{2,1,0:T(8,128)(2,1)S(1)} %bitcast.28, bf16[16,4,1024]{2,0,1:T(8,128)(2,1)S(1)} %all-to-all-done.1), kind=kOutput, calls=%fused_computation | convolution fusion | flops 999161856 | bytes 61632512 | tf_op jit(solution)/shard_map/dot_general | solution.py:56
  91.9 28.0 %reduce_sum.12 = bf16[1024,7392]{0,1:T(8,128)(2,1)} reduce(bf16[4,1024,7392]{1,2,0:T(8,128)(2,1)} %convert_bitcast_fusion, bf16[]{:T(256)} %constant.34.clone.1), dimensions={0}, to_apply=%region_1.2 | reduce | flops 22708224 | bytes 75694080 | tf_op jit(solution)/shard_map/reduce_sum | solution.py:63
  119.9 0.0 collective-permute-done.3
  119.9 0.6 copy.19
  (8 shorter events, 0.1 us)
Async XLA Ops:
  7.2 55.7 %reduce-scatter.2.cloned.1.call-start = ((), (), s32[]{:S(2)}) async-start(), calls=%async_computation.3 | async-start | bytes 196608 | tf_op jit(solution)/shard_map/reduce_scatter | solution.py:14
  8.6 10.9 %collective-permute-start = (bf16[16,7392]{1,0:T(8,128)(2,1)S(1)}, bf16[16,7392]{1,0:T(8,128)(2,1)S(1)}, u32[]{:S(2)}, u32[]{:S(2)}) collective-permute-start(bf16[16,7392]{1,0:T(8,128)(2,1)S(1)} %fusion.10), channel_id=1, source_target_pairs={{0,1},{1,2},{2,3},{3,0},{4,5},{5,6},{6,7},{7,4},{8,9},{9,10},{10,1... | collective-permute-start | bytes 709640 | tf_op jit(solution)/shard_map/ppermute | solution.py:40
  19.5 8.7 %collective-permute-start.1 = (bf16[16,7392]{1,0:T(8,128)(2,1)S(1)}, bf16[16,7392]{1,0:T(8,128)(2,1)S(1)}, u32[]{:S(2)}, u32[]{:S(2)}) collective-permute-start(bf16[16,7392]{1,0:T(8,128)(2,1)S(1)} %collective-permute-done), channel_id=1, source_target_pairs={{0,1},{1,2},{2,3},{3,0},{4,5},{5,6},{6,7},{7,4},{8,9},{9,10},{10,1... | collective-permute-start | bytes 709640 | tf_op jit(solution)/shard_map/ppermute | solution.py:40
  28.3 7.9 %collective-permute-start.2 = (bf16[16,7392]{1,0:T(8,128)(2,1)S(1)}, bf16[16,7392]{1,0:T(8,128)(2,1)S(1)}, u32[]{:S(2)}, u32[]{:S(2)}) collective-permute-start(bf16[16,7392]{1,0:T(8,128)(2,1)S(1)} %collective-permute-done.1), channel_id=1, source_target_pairs={{0,1},{1,2},{2,3},{3,0},{4,5},{5,6},{6,7},{7,4},{8,9},{9,10},{10,1... | collective-permute-start | bytes 709640 | tf_op jit(solution)/shard_map/ppermute | solution.py:40
  36.4 17.1 %copy-start = (bf16[1,1,8,4096]{3,2,1,0:T(8,128)(2,1)S(1)}, bf16[1,1,8,4096]{3,2,1,0:T(8,128)(2,1)}, u32[]{:S(2)}) copy-start(bf16[1,1,8,4096]{3,2,1,0:T(8,128)(2,1)} %param.5) | copy-start | bytes 196612
  59.2 9.2 %all-to-all-start.1 = ((bf16[16,4,1024]{2,0,1:T(8,128)(2,1)}), bf16[16,4,1024]{2,0,1:T(8,128)(2,1)S(1)}, u32[]{:S(2)}, u32[]{:S(2)}) async-start(bf16[16,4,1024]{2,0,1:T(8,128)(2,1)} %copy.9), calls=%async_computation.2 | async-start | bytes 262144 | tf_op jit(solution)/shard_map/all_to_all | solution.py:55
  62.9 57.0 %collective-permute-start.3 = (bf16[8,4096]{1,0:T(8,128)(2,1)}, bf16[8,4096]{1,0:T(8,128)(2,1)S(1)}, u32[]{:S(2)}, u32[]{:S(2)}) collective-permute-start(bf16[8,4096]{1,0:T(8,128)(2,1)} %reduce-scatter.2.cloned.1.call-done), channel_id=1, source_target_pairs={{8,0},{16,8},{24,16},{9,1},{17,9},{25,17},{10,2},{18,10},{26,18},{... | collective-permute-start | bytes 196616 | tf_op jit(solution)/shard_map/ppermute | solution.py:10
Sparse Core Ops, SparseCore 0:
  53.7 9.2 reduce-scatter.1
